TPU v7x, 32 devices: a whole 2x2x4 slice. The times are simulated.
32 devices in a mesh: dp: 2 (over y), row: 4 (over x, core), col: 4 (over z).
Axes of the slice: x: 2, y: 2, z: 4, core: 2. Of those that a mesh axis runs over, the one named last changes fastest.
Arguments:
- tokens: bfloat16 [2048, 8192], P(('dp', 'col'), 'row'), may hold values from -6 to 6
- frozen_weight: bfloat16 [8192, 8192], P('row', 'col'), may hold values from -0.0625 to 0.0625
- input_adapter_factor: bfloat16 [16, 8192], P(None, 'row'), may hold values from -0.0625 to 0.0625
- output_adapter_factor: bfloat16 [16, 8192], P(None, 'col'), may hold values from -1.5 to 1.5
- magnitude: float32 [8192], P('col'), may hold values from 0.5 to 2
- cotangent: bfloat16 [2048, 8192], P(('dp', 'row'), 'col'), may hold values from -6 to 6
- sequence_lengths: int32 [2, 8], P('dp'), may hold values from 1 to 512, 1024 in all within a row
Outputs:
- projected: bfloat16 [2048, 8192], P(('dp', 'row'), 'col')
- grad_mag: float32 [8192], P('col')
- input_factor_gradient: float32 [16, 8192], P(None, 'row')
- grad_b: float32 [16, 8192], P(None, 'col')
Inputs may be any that keep to these rules, and one draw needn't show every extreme that they name: `sequence_lengths`: each group's 8 lengths sum to 1024, and one of them is exactly 512.
All inputs are finite; a program needn't handle non-finite values.
Results may differ from a plain program's by a relative error of at most 0.0052.
Values may be sent and summed in bfloat16 or wider, within the bound.
No kernel may reach another device: no remote copies, remote signals or barrier semaphores. Data moves between devices by JAX's collectives and lax.ppermute only.
A program may use at most 64 MiB of HBM per device.

v0:
```python
import jax
import jax.numpy as jnp
from jax import lax
from jax.sharding import PartitionSpec as P

norm_eps = 1e-06
highest_precision = lax.Precision.HIGHEST


def contract_product(left, right, left_dim, right_dim):
    return lax.dot_general(
        left, right, (((left_dim,), (right_dim,)), ((), ())), preferred_element_type=jnp.float32
    )


def per_device(
    tokens,
    frozen_weight,
    input_adapter_factor,
    output_adapter_factor,
    magnitude,
    cotangent,
    sequence_lengths,
):
    row_count = lax.axis_size("row")
    col_count = lax.axis_size("col")
    row_index = lax.axis_index("row")
    col_index = lax.axis_index("col")
    group_index = lax.axis_index("dp")
    local_rows = tokens.shape[0]
    group_rows = local_rows * col_count
    block_rows = group_rows // row_count
    adapter_rank_size = input_adapter_factor.shape[0]
    low_rank_update = contract_product(input_adapter_factor, output_adapter_factor, 0, 0)
    merged = frozen_weight.astype(jnp.float32) + low_rank_update
    norm_terms = jnp.sum(merged * merged, axis=0)
    gram_partial_terms = contract_product(input_adapter_factor, input_adapter_factor, 1, 1)
    merged_factor_terms = jnp.dot(
        input_adapter_factor, frozen_weight, preferred_element_type=jnp.float32
    ) + jnp.dot(
        gram_partial_terms, output_adapter_factor.astype(jnp.float32), precision=highest_precision
    )
    portion = lax.all_gather(tokens, "col", axis=0, tiled=True)
    base_piece = jnp.dot(portion, frozen_weight, preferred_element_type=jnp.float32)
    down_portion = contract_product(portion, input_adapter_factor, 1, 1)
    frozen_rows, down_rows = (
        lax.psum_scatter(base_piece, "row", scatter_dimension=0, tiled=True),
        lax.psum_scatter(down_portion, "row", scatter_dimension=0, tiled=True),
    )
    norm_sq, merged_input_factor = lax.psum((norm_terms, merged_factor_terms), "row")
    down_activations = down_rows.astype(jnp.bfloat16)
    col_norm = jnp.sqrt(norm_sq + norm_eps)
    col_scale = magnitude / col_norm
    query_projection = frozen_rows + jnp.dot(
        down_activations, output_adapter_factor, preferred_element_type=jnp.float32
    )
    projected = (query_projection * col_scale[None, :]).astype(jnp.bfloat16)
    lengths = sequence_lengths[0]
    ends = jnp.cumsum(lengths, dtype=jnp.int32)
    starts = ends - lengths
    positions = row_index * block_rows + jnp.arange(block_rows, dtype=jnp.int32)
    inside = (positions[:, None] >= starts[None, :]) & (positions[:, None] < ends[None, :])
    inverse = 1.0 / lengths.astype(jnp.float32)
    weights = jnp.sum(jnp.where(inside, inverse[None, :], jnp.float32(0.0)), axis=1)
    grad_out = cotangent.astype(jnp.float32) * weights[:, None]
    scale_terms = jnp.sum(grad_out * query_projection, axis=0)
    projection_gradient = (grad_out * col_scale[None, :]).astype(jnp.bfloat16)
    bgrad_terms = contract_product(down_activations, projection_gradient, 0, 0)
    scale_grad, bgrad_data = lax.psum((scale_terms, bgrad_terms), ("dp", "row"))
    grad_mag = scale_grad / col_norm
    norm_coefficient = -scale_grad * magnitude / (col_norm * col_norm * col_norm)
    grad_b = bgrad_data + merged_input_factor * norm_coefficient[None, :]
    backward_terms = contract_product(projection_gradient, output_adapter_factor, 1, 1)
    padded = lax.dynamic_update_slice_in_dim(
        jnp.zeros((group_rows, adapter_rank_size), jnp.float32),
        backward_terms,
        row_index * block_rows,
        0,
    )
    backward_rows = lax.psum(padded, ("row", "col")).astype(jnp.bfloat16)
    back_mine = lax.dynamic_slice_in_dim(backward_rows, col_index * local_rows, local_rows, 0)
    row_term = contract_product(back_mine, tokens, 0, 0)
    scaled_output_factor = (
        output_adapter_factor.astype(jnp.float32) * norm_coefficient[None, :]
    ).astype(jnp.bfloat16)
    norm_term = contract_product(scaled_output_factor, frozen_weight, 1, 1) + jnp.dot(
        contract_product(scaled_output_factor, output_adapter_factor, 1, 1),
        input_adapter_factor.astype(jnp.float32),
        precision=highest_precision,
    )
    first_group = (group_index == 0).astype(jnp.float32)
    input_factor_gradient = lax.psum(row_term + first_group * norm_term, ("dp", "col"))
    return (projected, grad_mag, input_factor_gradient, grad_b)


def solution(mesh):
    in_specs = (
        P(("dp", "col"), "row"),
        P("row", "col"),
        P(None, "row"),
        P(None, "col"),
        P("col"),
        P(("dp", "row"), "col"),
        P("dp", None),
    )
    out_specs = (P(("dp", "row"), "col"), P("col"), P(None, "row"), P(None, "col"))
    return jax.shard_map(
        per_device, mesh=mesh, in_specs=in_specs, out_specs=out_specs, check_vma=False
    )
```

profile of v0, /device:TPU:0, one launch (start us, length us, event | category | flops | bytes accessed | tf_op | source)
XLA Modules:
  0.0 366.2 jit_solution(13270679273868545477)
XLA Ops:
  7.2 0.0 copy-start
  7.2 0.0 all-gather.2.cloned.1.call-start
  7.2 0.7 all-gather.2.cloned.1.call-update
  7.9 0.0 reduce-scatter.5.cloned.1.call-start
  8.0 85.1 %all-gather.2.cloned.1.call-done = bf16[1024,2048]{1,0:T(8,128)(2,1)} async-done(((bf16[256,2048]{1,0:T(8,128)(2,1)}), bf16[1024,2048]{1,0:T(8,128)(2,1)}) %all-gather.2.cloned.1.call-update) | async-done | bytes 4194320 | tf_op jit(solution)/shard_map/all_gather | solution.py:43
  93.1 0.0 copy-done
  93.1 4.0 %fusion.14 = f32[1024,16]{0,1:T(8,128)} fusion(bf16[1024,2048]{1,0:T(8,128)(2,1)} %all-gather.2.cloned.1.call-done, bf16[16,2048]{1,0:T(8,128)(2,1)S(1)} %copy-done), kind=kOutput, calls=%fused_computation.33 | convolution fusion | flops 67108864 | bytes 4325376 | tf_op jit(solution)/shard_map/dot_general | solution.py:11
  97.1 0.0 reduce-scatter.5.cloned.1.call-update
  97.1 0.0 reduce-scatter.3.cloned.1.call-start
  97.1 14.4 %fusion.13 = f32[1024,2048]{1,0:T(8,128)} fusion(bf16[1024,2048]{1,0:T(8,128)(2,1)} %all-gather.2.cloned.1.call-done, bf16[2048,2048]{1,0:T(8,128)(2,1)} %param.8), kind=kOutput, calls=%fused_computation.32 | convolution fusion | flops 8589934592 | bytes 20971520 | tf_op jit(solution)/shard_map/dot_general | solution.py:44
  111.6 0.0 reduce-scatter.3.cloned.1.call-update
  111.6 0.0 all-reduce.8.cloned.1.call-start
  111.6 0.1 fusion.16
  111.8 4.6 %fusion.15 = f32[16,2048]{1,0:T(8,128)S(1)} fusion(bf16[16,2048]{1,0:T(8,128)(2,1)S(1)} %copy-done, bf16[2048,2048]{1,0:T(8,128)(2,1)} %param.8), kind=kOutput, calls=%fused_computation.34 | convolution fusion | flops 134217728 | bytes 8585216 | tf_op jit(solution)/shard_map/dot_general | solution.py:38
  116.4 0.0 copy-done.2
  116.4 0.9 convolution_add_fusion.1
  117.3 0.0 all-reduce.8.cloned.1.call-update
  117.3 0.0 all-reduce.6.cloned.1.call-start
  117.3 0.0 copy-start.5
  117.4 0.0 copy-start.4
  117.4 0.0 copy-start.3
  117.4 5.9 %multiply_reduce_fusion = f32[2048]{0:T(1024)S(1)} fusion(bf16[2048,2048]{1,0:T(8,128)(2,1)} %param.8, bf16[16,2048]{1,0:T(8,128)(2,1)S(1)} %copy-done, bf16[16,2048]{1,0:T(8,128)(2,1)S(1)} %copy-done.2), kind=kOutput, calls=%fused_computation | convolution fusion | flops 150992896 | bytes 8527872 | tf_op jit(solution)/shard_map/dot_general | solution.py:11
  123.3 0.0 copy-done.5
  123.3 0.2 reduce-window.4
  123.5 6.5 %psum.42 = f32[2048]{0:T(1024)S(1)} all-reduce(f32[2048]{0:T(1024)S(1)} %multiply_reduce_fusion), channel_id=1, replica_groups=mesh['dp'=2,'row'=4,'col'=4] {'row'}, use_global_device_ids=true, to_apply=%region_3.0 | all-reduce | flops 2048 | bytes 16384 | tf_op jit(solution)/shard_map/psum | solution.py:50
  130.0 0.0 copy-done.4
  130.1 0.1 select_reduce_fusion
  130.2 0.5 convolution_dynamic-update-slice_fusion
  130.7 69.2 %psum.44 = bf16[1024,16]{1,0:T(8,128)(2,1)S(1)} all-reduce(f32[1024,16]{1,0:T(8,128)S(1)} %convolution_dynamic-update-slice_fusion), channel_id=1, replica_groups=mesh['dp'=2,'row'=4,'col'=4] {'row','col'}, use_global_device_ids=true, to_apply=%region_8.9 | all-reduce | flops 16384 | bytes 98304 | tf_op jit(solution)/shard_map/psum | solution.py:80
  199.9 0.0 reduce-scatter.5.cloned.1.call-done
  200.0 1.8 fusion.1
  201.8 0.0 all-reduce.6.cloned.1.call-update
  201.8 0.0 all-reduce.4.cloned.1.call-start
  201.8 0.0 reduce-scatter.3.cloned.1.call-done
  201.9 3.2 multiply_reduce_fusion.1
  205.1 12.1 %psum.43 = f32[2048]{0:T(1024)S(1)} all-reduce(f32[2048]{0:T(1024)S(1)} %get-tuple-element.4), channel_id=1, replica_groups=mesh['dp'=2,'row'=4,'col'=4] {'dp','row'}, use_global_device_ids=true, to_apply=%region_7.8 | all-reduce | flops 2048 | bytes 16384 | tf_op jit(solution)/shard_map/psum | solution.py:69
  217.1 0.6 fusion.6
  217.8 5.7 %fusion.3 = f32[16,2048]{1,0:T(8,128)S(1)} fusion(bf16[2048,2048]{1,0:T(8,128)(2,1)} %param.8, bf16[16,2048]{1,0:T(8,128)(2,1)S(1)} %copy-done.2, f32[2048]{0:T(1024)S(1)} %get-tuple-element.6), kind=kOutput, calls=%fused_computation.16 | convolution fusion | flops 134316032 | bytes 8593408 | tf_op jit(solution)/shard_map/dot_general | solution.py:11
  223.5 0.1 fusion.2
  223.6 0.2 fusion
  223.9 0.0 copy-done.1
  223.9 0.9 convolution_add_fusion.3
  224.8 0.0 all-reduce.4.cloned.1.call-update
  224.8 2.4 all-reduce.8.cloned.1.call-done
  227.2 57.0 %all-reduce.6.cloned.1.call-done = f32[16,2048]{1,0:T(8,128)} async-done(((f32[16,2048]{1,0:T(8,128)}), f32[16,2048]{1,0:T(8,128)}) %all-reduce.6.cloned.1.call-update) | async-done | bytes 131088 | tf_op jit(solution)/shard_map/psum | solution.py:69
  284.2 1.6 multiply_add_fusion
  285.9 71.9 %all-reduce.4.cloned.1.call-done = f32[16,2048]{1,0:T(8,128)} async-done(((f32[16,2048]{1,0:T(8,128)}), f32[16,2048]{1,0:T(8,128)}) %all-reduce.4.cloned.1.call-update) | async-done | bytes 131088 | tf_op jit(solution)/shard_map/psum | solution.py:92
  357.8 1.6 copy.15
  (8 shorter events, 0.1 us)
Async XLA Ops:
  7.2 85.9 %copy-start = (bf16[16,2048]{1,0:T(8,128)(2,1)S(1)}, bf16[16,2048]{1,0:T(8,128)(2,1)}, u32[]{:S(2)}) copy-start(bf16[16,2048]{1,0:T(8,128)(2,1)} %param.9) | copy-start | bytes 196612
  7.2 85.9 %all-gather.2.cloned.1.call-start = ((), (), s32[]{:S(2)}) async-start(), calls=%async_computation.2 | async-start | bytes 5242880 | tf_op jit(solution)/shard_map/all_gather | solution.py:43
  7.9 192.0 %reduce-scatter.5.cloned.1.call-start = ((), (), s32[]{:S(2)}) async-start(), calls=%async_computation.4 | async-start | bytes 81920 | tf_op jit(solution)/shard_map/reduce_scatter | solution.py:48
  97.1 104.8 %reduce-scatter.3.cloned.1.call-start = ((), (), s32[]{:S(2)}) async-start(), calls=%async_computation.3 | async-start | bytes 10485760 | tf_op jit(solution)/shard_map/reduce_scatter | solution.py:47
  111.6 115.7 %all-reduce.8.cloned.1.call-start = ((), (), s32[]{:S(2)}) async-start(), calls=%async_computation.7 | async-start | bytes 262144 | tf_op jit(solution)/shard_map/psum | solution.py:50
  111.8 4.6 %copy-start.2 = (bf16[16,2048]{1,0:T(8,128)(2,1)S(1)}, bf16[16,2048]{1,0:T(8,128)(2,1)}, u32[]{:S(2)}) copy-start(bf16[16,2048]{1,0:T(8,128)(2,1)} %param.10) | copy-start | bytes 196612
  117.3 166.9 %all-reduce.6.cloned.1.call-start = ((), (), s32[]{:S(2)}) async-start(), calls=%async_computation.6 | async-start | bytes 262144 | tf_op jit(solution)/shard_map/psum | solution.py:69
  117.3 5.9 %copy-start.5 = (s32[1,8]{1,0:T(1,128)S(1)}, s32[1,8]{1,0:T(1,128)}, u32[]{:S(2)}) copy-start(s32[1,8]{1,0:T(1,128)} %param.13) | copy-start | bytes 100
  117.4 12.7 %copy-start.4 = (f32[2048]{0:T(1024)S(1)}, f32[2048]{0:T(1024)}, u32[]{:S(2)}) copy-start(f32[2048]{0:T(1024)} %param.11) | copy-start | bytes 24580
  117.4 12.8 %copy-start.3 = (bf16[256,2048]{1,0:T(8,128)(2,1)S(1)}, bf16[256,2048]{1,0:T(8,128)(2,1)}, u32[]{:S(2)}) copy-start(bf16[256,2048]{1,0:T(8,128)(2,1)} %param.12) | copy-start | bytes 3145732
  201.8 156.0 %all-reduce.4.cloned.1.call-start = ((), (), s32[]{:S(2)}) async-start(), calls=%async_computation.5 | async-start | bytes 262144 | tf_op jit(solution)/shard_map/psum | solution.py:92
  217.8 6.1 %copy-start.1 = (bf16[256,2048]{1,0:T(8,128)(2,1)S(1)}, bf16[256,2048]{1,0:T(8,128)(2,1)}, u32[]{:S(2)}) copy-start(bf16[256,2048]{1,0:T(8,128)(2,1)} %param.7) | copy-start | bytes 3145732
Sparse Core Ops, SparseCore 0:
  9.6 83.4 all-gather.1
  97.2 18.0 reduce-scatter.4
  117.9 75.6 reduce-scatter.2
  195.8 31.4 all-reduce.7
  230.7 53.4 all-reduce.5
  288.0 69.7 all-reduce.3
where the time goes:
time: 367 us; the launch traced here: 366 us
  waiting for transfers between devices  217 us (59%)
  blocking collectives  87.8 us (24%)
  matrix products  42.5 us (12%)
  between operations  14.3 us (4%)
    all_gather x1, waiting for transfers between devices, per_device(): portion = lax.all_gather(tokens, 'col', axis=0, tiled=True)  85.1 us
    psum x1, waiting for transfers between devices, per_device(): lax.psum(row_term + first_group * norm_term, ('dp', 'col'))  71.9 us
    psum x1, blocking collectives, per_device(): backward_rows = lax.psum(padded, ('row', 'col')).astype(jnp.bfloat16)  69.2 us
    psum x1, waiting for transfers between devices, per_device(): scale_grad, bgrad_data = lax.psum((scale_terms, bgrad_terms), ('dp', 'row'))  57 us
    dot_general x8, matrix products, contract_product(): lax.dot_general(left, right, (((left_dim,), (right_dim,)), ((), ())), pre...  19.1 us
    dot_general x1, matrix products, per_device(): jnp.dot(portion, frozen_weight, preferred_element_type=jnp.float32)  14.4 us
    psum x1, blocking collectives, per_device(): scale_grad, bgrad_data = lax.psum((scale_terms, bgrad_terms), ('dp', 'row'))  12.1 us
  transfers between devices with their start and end apart: 6, of which 4 were waited for; matrix products, arithmetic and copies ran while one was open for 11% of the time, Pallas kernels for 0%

commit v1 on v0

--- a/solution.py
+++ b/solution.py
@@ -5,6 +5,17 @@
 
 norm_eps = 1e-06
 highest_precision = lax.Precision.HIGHEST
+
+
+def around_the_ring(array, axis, along):
+    peers = lax.axis_size(axis)
+    right = [(i, (i + 1) % peers) for i in range(peers)]
+    parts = [array]
+    for stride in range(1, peers):
+        parts = [lax.ppermute(parts[0], axis, right), *parts]
+    out = jnp.concatenate(parts, axis=along)
+    offset = (lax.axis_index(axis) + 1) * parts[-1].shape[along]
+    return jnp.roll(out, offset, axis=along)
 
 
 def contract_product(left, right, left_dim, right_dim):
@@ -40,7 +51,7 @@
     ) + jnp.dot(
         gram_partial_terms, output_adapter_factor.astype(jnp.float32), precision=highest_precision
     )
-    portion = lax.all_gather(tokens, "col", axis=0, tiled=True)
+    portion = around_the_ring(tokens, "col", 0)
     base_piece = jnp.dot(portion, frozen_weight, preferred_element_type=jnp.float32)
     down_portion = contract_product(portion, input_adapter_factor, 1, 1)
     frozen_rows, down_rows = (

time: 367 us -> 366 us (level)
  waiting for transfers between devices: 217 us -> 207 us
  local copies, waits for them, and re-layouts: 1.64 us -> 9.21 us
  other arithmetic: 2.55 us -> 7.32 us
  matrix products: 42.5 us -> 38.1 us
    all_gather x1 -> x0, waiting for transfers between devices: 85.1 us -> none  [per_device(): portion = lax.all_gather(tokens, 'col', axis=0, tiled=True)]
    ppermute x0 -> x3, waiting for transfers between devices: none -> 76.9 us  [around_the_ring(): parts = [lax.ppermute(parts[0], axis, right), *parts]]
    unnamed x13 -> x24, local copies, waits for them, and re-layouts: 1.6 us -> 9.11 us
    reduce_sum x0 -> x1, other arithmetic: none -> 4.07 us  [per_device(): scale_terms = jnp.sum(grad_out * query_projection, axis=0)]
  transfers between devices with their start and end apart: 6 -> 8, of which waited for: 4 -> 6; matrix products, arithmetic and copies ran while one was open for 11% -> 12% of each run, Pallas kernels for 0% -> 0%
where the time goes in v1:
time: 366 us; the launch traced here: 365 us
  waiting for transfers between devices  207 us (57%)
  blocking collectives  86.4 us (24%)
  matrix products  38.1 us (10%)
  between operations  14 us (4%)
  local copies, waits for them, and re-layouts  9.21 us (3%)
  other arithmetic  7.32 us (2%)
    ppermute x3, waiting for transfers between devices, around_the_ring(): parts = [lax.ppermute(parts[0], axis, right), *parts]  76.9 us
    psum x1, waiting for transfers between devices, per_device(): lax.psum(row_term + first_group * norm_term, ('dp', 'col'))  71.9 us
    psum x1, blocking collectives, per_device(): backward_rows = lax.psum(padded, ('row', 'col')).astype(jnp.bfloat16)  68.5 us
    psum x1, waiting for transfers between devices, per_device(): scale_grad, bgrad_data = lax.psum((scale_terms, bgrad_terms), ('dp', 'row'))  56.9 us
    dot_general x8, matrix products, contract_product(): lax.dot_general(left, right, (((left_dim,), (right_dim,)), ((), ())), pre...  16.8 us
    dot_general x1, matrix products, per_device(): jnp.dot(portion, frozen_weight, preferred_element_type=jnp.float32)  14.4 us
    psum x1, blocking collectives, per_device(): scale_grad, bgrad_data = lax.psum((scale_terms, bgrad_terms), ('dp', 'row'))  12.1 us
    unnamed x24, local copies, waits for them, and re-layouts  9.11 us
  transfers between devices with their start and end apart: 8, of which 6 were waited for; matrix products, arithmetic and copies ran while one was open for 12% of the time, Pallas kernels for 0%

profile of v1, /device:TPU:0, one launch (start us, length us, event | category | flops | bytes accessed | tf_op | source)
XLA Modules:
  0.0 364.9 jit_solution(3720067078393233731)
XLA Ops:
  7.2 0.0 reduce-scatter.5.cloned.1.call-start
  7.2 3.1 collective-permute-start
  10.3 25.4 %collective-permute-done = bf16[256,2048]{1,0:T(8,128)(2,1)S(1)} collective-permute-done((bf16[256,2048]{1,0:T(8,128)(2,1)}, bf16[256,2048]{1,0:T(8,128)(2,1)S(1)}, u32[]{:S(2)}, u32[]{:S(2)}) %collective-permute-start) | collective-permute-done | bytes 1048608 | tf_op jit(solution)/shard_map/ppermute | solution.py:15
  35.7 26.1 %collective-permute-done.1 = bf16[256,2048]{1,0:T(8,128)(2,1)S(1)} collective-permute-done((bf16[256,2048]{1,0:T(8,128)(2,1)S(1)}, bf16[256,2048]{1,0:T(8,128)(2,1)S(1)}, u32[]{:S(2)}, u32[]{:S(2)}) %collective-permute-start.1) | collective-permute-done | bytes 1048608 | tf_op jit(solution)/shard_map/ppermute | solution.py:15
  61.9 25.4 %collective-permute-done.2 = bf16[256,2048]{1,0:T(8,128)(2,1)} collective-permute-done((bf16[256,2048]{1,0:T(8,128)(2,1)S(1)}, bf16[256,2048]{1,0:T(8,128)(2,1)}, u32[]{:S(2)}, u32[]{:S(2)}) %collective-permute-start.2) | collective-permute-done | bytes 1048608 | tf_op jit(solution)/shard_map/ppermute | solution.py:15
  87.2 1.3 constant_dynamic-update-slice_fusion.7
  88.5 0.1 constant_dynamic-update-slice_fusion.6
  88.6 0.1 constant_dynamic-update-slice_fusion.5
  88.7 1.3 constant_dynamic-update-slice_fusion.4
  90.1 1.3 constant_dynamic-update-slice_fusion.3
  91.3 0.1 constant_dynamic-update-slice_fusion.2
  91.5 0.1 constant_dynamic-update-slice_fusion.1
  91.6 0.1 constant_dynamic-update-slice_fusion
  91.7 3.2 copy-done.4
  94.9 1.8 fusion
  96.7 0.0 reduce-scatter.5.cloned.1.call-update
  96.7 0.0 reduce-scatter.3.cloned.1.call-start
  96.8 14.4 %fusion.2 = f32[1024,2048]{1,0:T(8,128)} fusion(bf16[2048,2048]{1,0:T(8,128)(2,1)} %param.8, bf16[2048,2048]{1,0:T(8,128)(2,1)} %copy-done.4, s32[]{:T(128)S(6)} %select_n.24), kind=kOutput, calls=%fused_computation.3 | convolution fusion | flops 8589934592 | bytes 20971524 | tf_op jit(solution)/shard_map/dot_general | solution.py:55
  111.2 0.0 reduce-scatter.3.cloned.1.call-update
  111.3 0.0 all-reduce.8.cloned.1.call-start
  111.3 0.1 fusion.21
  111.4 4.6 %fusion.20 = f32[16,2048]{1,0:T(8,128)S(1)} fusion(bf16[16,2048]{1,0:T(8,128)(2,1)S(1)} %copy-done, bf16[2048,2048]{1,0:T(8,128)(2,1)} %param.8), kind=kOutput, calls=%fused_computation.46 | convolution fusion | flops 134217728 | bytes 8585216 | tf_op jit(solution)/shard_map/dot_general | solution.py:49
  116.1 0.9 convolution_add_fusion
  116.9 0.0 all-reduce.8.cloned.1.call-update
  117.0 0.0 all-reduce.6.cloned.1.call-start
  117.0 5.9 %multiply_reduce_fusion = f32[2048]{0:T(1024)S(1)} fusion(bf16[2048,2048]{1,0:T(8,128)(2,1)} %param.8, bf16[16,2048]{1,0:T(8,128)(2,1)S(1)} %copy-done, bf16[16,2048]{1,0:T(8,128)(2,1)S(1)} %copy-done.2), kind=kOutput, calls=%fused_computation | convolution fusion | flops 150992896 | bytes 8527872 | tf_op jit(solution)/shard_map/dot_general | solution.py:22
  122.9 0.2 reduce-window.4
  123.1 5.7 %psum.42 = f32[2048]{0:T(1024)S(1)} all-reduce(f32[2048]{0:T(1024)S(1)} %multiply_reduce_fusion), channel_id=1, replica_groups=mesh['dp'=2,'row'=4,'col'=4] {'row'}, use_global_device_ids=true, to_apply=%region_3.4 | all-reduce | flops 2048 | bytes 16384 | tf_op jit(solution)/shard_map/psum | solution.py:61
  128.9 0.1 select_reduce_fusion
  129.0 0.5 convolution_dynamic-update-slice_fusion
  129.5 68.5 %psum.44 = bf16[1024,16]{1,0:T(8,128)(2,1)S(1)} all-reduce(f32[1024,16]{1,0:T(8,128)S(1)} %convolution_dynamic-update-slice_fusion), channel_id=1, replica_groups=mesh['dp'=2,'row'=4,'col'=4] {'row','col'}, use_global_device_ids=true, to_apply=%region_8.9 | all-reduce | flops 16384 | bytes 98304 | tf_op jit(solution)/shard_map/psum | solution.py:91
  198.0 0.0 reduce-scatter.5.cloned.1.call-done
  198.1 1.8 fusion.5
  199.9 0.0 all-reduce.4.cloned.1.call-start
  199.9 1.2 fusion.14
  201.1 0.0 reduce-scatter.3.cloned.1.call-done
  201.1 4.1 %multiply_reduce_fusion.1 = (f32[2048]{0:T(1024)}, bf16[256,2048]{1,0:T(8,128)(2,1)}) fusion(bf16[256,2048]{1,0:T(8,128)(2,1)} %param.12, f32[256]{0:T(256)} %copy-done.6, f32[256,2048]{1,0:T(8,128)} %reduce-scatter.3.cloned.1.call-done, f32[256,2048]{1,0:T(8,128)S(1)} %fusion.14, f32[2048]{0:T(1024)S(1)} %fusion.12), kind=kLoop, calls=%fused_computation.10 | loop fusion | flops 3667968 | bytes 6308864 | tf_op jit(solution)/shard_map/reduce_sum | solution.py:77
  205.2 12.1 %psum.43 = f32[2048]{0:T(1024)S(1)} all-reduce(f32[2048]{0:T(1024)} %get-tuple-element.4), channel_id=1, replica_groups=mesh['dp'=2,'row'=4,'col'=4] {'dp','row'}, use_global_device_ids=true, to_apply=%region_7.8 | all-reduce | flops 2048 | bytes 16384 | tf_op jit(solution)/shard_map/psum | solution.py:80
  217.4 1.3 fusion.10
  218.7 5.7 %fusion.7 = f32[16,2048]{1,0:T(8,128)S(1)} fusion(bf16[2048,2048]{1,0:T(8,128)(2,1)} %param.8, bf16[16,2048]{1,0:T(8,128)(2,1)S(1)} %copy-done.2, f32[2048]{0:T(1024)S(1)} %get-tuple-element.6), kind=kOutput, calls=%fused_computation.19 | convolution fusion | flops 134316032 | bytes 8593408 | tf_op jit(solution)/shard_map/dot_general | solution.py:22
  224.3 0.1 fusion.6
  224.5 0.2 fusion.4
  224.7 0.9 convolution_add_fusion.2
  225.7 0.7 all-reduce.8.cloned.1.call-done
  226.3 56.9 %all-reduce.6.cloned.1.call-done = f32[16,2048]{1,0:T(8,128)} async-done(((f32[16,2048]{1,0:T(8,128)}), f32[16,2048]{1,0:T(8,128)}) %all-reduce.6.cloned.1.call-update) | async-done | bytes 131088 | tf_op jit(solution)/shard_map/psum | solution.py:80
  283.3 1.6 multiply_add_fusion
  284.9 71.9 %all-reduce.4.cloned.1.call-done = f32[16,2048]{1,0:T(8,128)} async-done(((f32[16,2048]{1,0:T(8,128)}), f32[16,2048]{1,0:T(8,128)}) %all-reduce.4.cloned.1.call-update) | async-done | bytes 131088 | tf_op jit(solution)/shard_map/psum | solution.py:103
  356.8 1.6 copy.22
  (24 shorter events, 0.1 us)
Async XLA Ops:
  7.2 87.7 %copy-start = (bf16[16,2048]{1,0:T(8,128)(2,1)S(1)}, bf16[16,2048]{1,0:T(8,128)(2,1)}, u32[]{:S(2)}) copy-start(bf16[16,2048]{1,0:T(8,128)(2,1)} %param.9) | copy-start | bytes 196612
  7.2 84.4 %copy-start.1 = (bf16[256,2048]{1,0:T(8,128)(2,1)S(1)}, bf16[256,2048]{1,0:T(8,128)(2,1)}, u32[]{:S(2)}) copy-start(bf16[256,2048]{1,0:T(8,128)(2,1)} %param.7) | copy-start | bytes 3145732
  7.2 190.9 %reduce-scatter.5.cloned.1.call-start = ((), (), s32[]{:S(2)}) async-start(), calls=%async_computation.3 | async-start | bytes 81920 | tf_op jit(solution)/shard_map/reduce_scatter | solution.py:59
  7.2 28.5 %collective-permute-start = (bf16[256,2048]{1,0:T(8,128)(2,1)}, bf16[256,2048]{1,0:T(8,128)(2,1)S(1)}, u32[]{:S(2)}, u32[]{:S(2)}) collective-permute-start(bf16[256,2048]{1,0:T(8,128)(2,1)} %param.7), channel_id=1, source_target_pairs={{0,1},{1,2},{2,3},{3,0},{4,5},{5,6},{6,7},{7,4},{8,9},{9,10},{10,1... | collective-permute-start | bytes 3145736 | tf_op jit(solution)/shard_map/ppermute | solution.py:15
  35.7 26.1 %collective-permute-start.1 = (bf16[256,2048]{1,0:T(8,128)(2,1)S(1)}, bf16[256,2048]{1,0:T(8,128)(2,1)S(1)}, u32[]{:S(2)}, u32[]{:S(2)}) collective-permute-start(bf16[256,2048]{1,0:T(8,128)(2,1)S(1)} %collective-permute-done), channel_id=1, source_target_pairs={{0,1},{1,2},{2,3},{3,0},{4,5},{5,6},{6,7},{7,4},{8,9},{9,10},{10,1... | collective-permute-start | bytes 3145736 | tf_op jit(solution)/shard_map/ppermute | solution.py:15
  61.9 25.4 %collective-permute-start.2 = (bf16[256,2048]{1,0:T(8,128)(2,1)S(1)}, bf16[256,2048]{1,0:T(8,128)(2,1)}, u32[]{:S(2)}, u32[]{:S(2)}) collective-permute-start(bf16[256,2048]{1,0:T(8,128)(2,1)S(1)} %collective-permute-done.1), channel_id=1, source_target_pairs={{0,1},{1,2},{2,3},{3,0},{4,5},{5,6},{6,7},{7,4},{8,9},{9,10},{10,1... | collective-permute-start | bytes 3145736 | tf_op jit(solution)/shard_map/ppermute | solution.py:15
  91.7 3.2 copy-start.4
  96.7 104.4 %reduce-scatter.3.cloned.1.call-start = ((), (), s32[]{:S(2)}) async-start(), calls=%async_computation.2 | async-start | bytes 10485760 | tf_op jit(solution)/shard_map/reduce_scatter | solution.py:58
  111.2 4.8 %copy-start.2 = (bf16[16,2048]{1,0:T(8,128)(2,1)S(1)}, bf16[16,2048]{1,0:T(8,128)(2,1)}, u32[]{:S(2)}) copy-start(bf16[16,2048]{1,0:T(8,128)(2,1)} %param.10) | copy-start | bytes 196612
  111.3 115.1 %all-reduce.8.cloned.1.call-start = ((), (), s32[]{:S(2)}) async-start(), calls=%async_computation.6 | async-start | bytes 262144 | tf_op jit(solution)/shard_map/psum | solution.py:61
  116.9 6.0 %copy-start.7 = (s32[1,8]{1,0:T(1,128)S(1)}, s32[1,8]{1,0:T(1,128)}, u32[]{:S(2)}) copy-start(s32[1,8]{1,0:T(1,128)} %param.13) | copy-start | bytes 100
  116.9 11.9 %copy-start.5 = (f32[2048]{0:T(1024)S(1)}, f32[2048]{0:T(1024)}, u32[]{:S(2)}) copy-start(f32[2048]{0:T(1024)} %param.11) | copy-start | bytes 24580
  117.0 12.1 %copy-start.3 = (bf16[256,2048]{1,0:T(8,128)(2,1)S(1)}, bf16[256,2048]{1,0:T(8,128)(2,1)}, u32[]{:S(2)}) copy-start(bf16[256,2048]{1,0:T(8,128)(2,1)} %param.12) | copy-start | bytes 3145732
  117.0 166.3 %all-reduce.6.cloned.1.call-start = ((), (), s32[]{:S(2)}) async-start(), calls=%async_computation.5 | async-start | bytes 262144 | tf_op jit(solution)/shard_map/psum | solution.py:80
  129.0 70.9 %copy-start.6 = (f32[256]{0:T(256)}, f32[256]{0:T(256)S(1)}, u32[]{:S(2)}) copy-start(f32[256]{0:T(256)S(1)} %select_reduce_fusion) | copy-start | bytes 3076
  199.9 156.9 %all-reduce.4.cloned.1.call-start = ((), (), s32[]{:S(2)}) async-start(), calls=%async_computation.4 | async-start | bytes 262144 | tf_op jit(solution)/shard_map/psum | solution.py:103
Sparse Core Ops, SparseCore 0:
  96.8 17.3 reduce-scatter.4
  116.8 75.6 reduce-scatter.2
  194.8 31.4 all-reduce.7
  229.8 53.4 all-reduce.5
  287.1 69.7 all-reduce.3
